TPU v7x, 32 devices: a whole 2x2x4 slice. The times are simulated.
32 devices in a mesh: leaf: 8 (over z, y), grid: 4 (over x, core).
Axes of the slice: x: 2, y: 2, z: 4, core: 2. Of those that a mesh axis runs over, the one named last changes fastest.
Arguments:
- source_leaf: float32 [8, 4096], P(None, ('leaf', 'grid')), may hold values from -6 to 6
- block_leaf: float32 [4096, 128], P(('leaf', 'grid')), may hold values from -0.5 to 0.5
- expand_leaf: float32 [4096, 128], P(('leaf', 'grid')), may hold values from -0.5 to 0.5
- basis_leaf: float32 [4096, 256], P(('leaf', 'grid')), may hold values from -0.25 to 0.25
- pivot_leaf: float32 [4096], P(('leaf', 'grid')), may hold values from -2 to 2
- couple_leaf: float32 [8192, 128], P(('leaf', 'grid')), may hold values from -0.5 to 0.5
- ranks_leaf: int32 [8, 2], replicated, may hold values from 32 to 128
- targets_leaf: int32 [8192], P(('leaf', 'grid')), may hold values from 0 to 2047, as said below
- source_middle: float32 [8, 4096], P(None, ('leaf', 'grid')), may hold values from -6 to 6
- block_middle: float32 [4096, 128], P(('leaf', 'grid')), may hold values from -0.5 to 0.5
- expand_middle: float32 [4096, 128], P(('leaf', 'grid')), may hold values from -0.5 to 0.5
- basis_middle: float32 [4096, 256], P(('leaf', 'grid')), may hold values from -0.1875 to 0.1875
- pivot_middle: float32 [4096], P(('leaf', 'grid')), may hold values from -2 to 2
- couple_middle: float32 [4096, 128], P(('leaf', 'grid')), may hold values from -0.5 to 0.5
- ranks_middle: int32 [4, 2], replicated, may hold values from 32 to 128
- targets_middle: int32 [4096], P(('leaf', 'grid')), may hold values from 0 to 4095, as said below
- source_upper: float32 [8, 4096], P(None, ('leaf', 'grid')), may hold values from -6 to 6
- block_upper: float32 [4096, 128], P(('leaf', 'grid')), may hold values from -0.5 to 0.5
- expand_upper: float32 [4096, 128], P(('leaf', 'grid')), may hold values from -0.5 to 0.5
- basis_upper: float32 [4096, 256], P(('leaf', 'grid')), may hold values from -0.125 to 0.125
- pivot_upper: float32 [4096], P(('leaf', 'grid')), may hold values from -2 to 2
- couple_upper: float32 [4096, 128], P(('leaf', 'grid')), may hold values from -0.5 to 0.5
- ranks_upper: int32 [2, 2], replicated, may hold values from 32 to 128
- targets_upper: int32 [4096], P(('leaf', 'grid')), may hold values from 0 to 4095, as said below
- source_root: float32 [8, 4096], P(None, ('leaf', 'grid')), may hold values from -6 to 6
- block_root: float32 [4096, 128], P(('leaf', 'grid')), may hold values from -0.5 to 0.5
- expand_root: float32 [4096, 128], P(('leaf', 'grid')), may hold values from -0.5 to 0.5
- basis_root: float32 [4096, 256], P(('leaf', 'grid')), may hold values from -0.09375 to 0.09375
- pivot_root: float32 [4096], P(('leaf', 'grid')), may hold values from -2 to 2
- ranks_root: int32 [1, 2], replicated, may hold values from 32 to 128
Outputs:
- answer_leaf: float32 [8, 4096], P(None, ('leaf', 'grid'))
- answer_middle: float32 [8, 4096], P(None, ('leaf', 'grid'))
- answer_upper: float32 [8, 4096], P(None, ('leaf', 'grid'))
- answer_root: float32 [8, 4096], P(None, ('leaf', 'grid'))
Inputs may be any that keep to these rules, and one draw needn't show every extreme that they name: `targets_leaf`: within one leaf front the 1024 entries are distinct; each names a row of the parent front's row vector of 2048 rows. Split that vector's separator part and its update part each evenly, in order, over the parent's devices (leaf then grid); then the rows of one device name at most 32 rows held by any one of them, and exactly that many for some. `targets_middle`: within one middle front the entries are distinct; each names a row of the parent front's row vector of 4096 rows. Split likewise over the parent's devices, the rows of one device name at most 8 rows held by any one of them, and exactly that many for some. `targets_upper`: within one upper front the entries are distinct; each names a row of the root separator. Split evenly in order over all devices, the rows of one device name at most 4 rows held by any one of them, and exactly that many for some.
All inputs are finite; a program needn't handle non-finite values.
Results may differ from a plain program's by a relative error of at most 0.0003.
Values sent between devices are 32-bit elements; how exact they have to be, the bound alone decides.
A program may use at most 128 MiB of HBM per device.

v0:
```python
import jax
import jax.numpy as jnp
from jax import lax
from jax.sharding import PartitionSpec as P

BLOCK = 128
RANK = 128
HIGH_PRECISION = lax.Precision.HIGHEST


def from_partner(value, axis, distance):
    mask = 2**distance
    pairs = [(source, source ^ mask) for source in range(lax.axis_size(axis))]
    return lax.ppermute(value, axis, pairs)


def mult(left, right):
    return jnp.dot(left, right, precision=HIGH_PRECISION, preferred_element_type=jnp.float32)


def inner(left, right):
    return lax.dot_general(
        left,
        right,
        (((0,), (0,)), ((), ())),
        precision=HIGH_PRECISION,
        preferred_element_type=jnp.float32,
    )


def outer(left, right):
    return lax.dot_general(
        left,
        right,
        (((1,), (1,)), ((), ())),
        precision=HIGH_PRECISION,
        preferred_element_type=jnp.float32,
    )


def paired_total(partial_value, bits):
    summed = lax.psum(partial_value, "grid")
    for bit in range(bits):
        summed = summed + from_partner(summed, "leaf", bit)
    return summed


def group_total(partial_value, bits):
    return paired_total(partial_value, bits)


def upper_bit(place, bit):
    return place // (1 << bit) % 2 == 1


def group_extend(stack, bits, place):
    for bit in reversed(range(bits)):
        half = stack.shape[2] // 2
        lower_part = stack[:, :, :half]
        upper_part = stack[:, :, half:]
        flag = upper_bit(place, bit)
        keep = jnp.where(flag, upper_part, lower_part)
        send = jnp.where(flag, lower_part, upper_part)
        stack = keep + from_partner(send, "leaf", bit)
    return lax.psum_scatter(stack, "grid", scatter_dimension=2, tiled=True)


def group_fetch(stack, bits, place):
    current = lax.all_gather(stack, "grid", axis=2, tiled=True)
    for bit in range(bits):
        other = from_partner(current, "leaf", bit)
        flag = upper_bit(place, bit)
        current = jnp.where(
            flag,
            jnp.concatenate([other, current], axis=2),
            jnp.concatenate([current, other], axis=2),
        )
    return current


def forward_level(source, incoming, block, expand, basis, pivot, ranks, bits, front):
    level_batch_index = source if incoming is None else source + incoming
    count, width = level_batch_index.shape
    tiles = block.reshape(width // BLOCK, BLOCK, BLOCK)
    local_portion = jnp.einsum(
        "anh,nhk->ank",
        level_batch_index.reshape(count, width // BLOCK, BLOCK),
        tiles,
        precision=HIGH_PRECISION,
    ).reshape(count, width)
    query_lookup = basis[:, :RANK]
    coupling_right_factor = basis[:, RANK:]
    rank_pair = lax.dynamic_index_in_dim(ranks, front, 0, keepdims=False)
    columns = jnp.arange(RANK, dtype=jnp.int32)
    head_mask_grid = (columns < rank_pair[0]).astype(jnp.float32)
    column_mask_grid = (columns < rank_pair[1]).astype(jnp.float32)
    partial_value = jnp.concatenate(
        [
            mult(level_batch_index, query_lookup),
            mult(local_portion, coupling_right_factor),
            inner(expand, coupling_right_factor),
        ],
        axis=0,
    )
    total = group_total(partial_value, bits)
    hidden_q = total[:count] * head_mask_grid
    cross = total[2 * count :]
    intermediate_entries = local_portion + outer(hidden_q, expand)
    weight_entries = (total[count : 2 * count] + mult(hidden_q, cross)) * column_mask_grid
    return (
        intermediate_entries * pivot[None, :],
        weight_entries,
        (tiles, query_lookup, coupling_right_factor, cross, head_mask_grid, column_mask_grid),
    )


def backward_level(correction_entries, x_upd, couple, expand, parts, bits):
    tiles, query_lookup, coupling_right_factor, cross, head_mask_grid, column_mask_grid = parts
    count, width = correction_entries.shape
    if x_upd is None:
        total = group_total(mult(correction_entries, expand), bits)
        remainder_rows = correction_entries
        right_projection = total * head_mask_grid
    else:
        total = group_total(
            jnp.concatenate([mult(x_upd, couple), mult(correction_entries, expand)], axis=0), bits
        )
        solve_direction = total[:count] * column_mask_grid
        remainder_rows = correction_entries - outer(solve_direction, coupling_right_factor)
        right_projection = (total[count:] - outer(solve_direction, cross)) * head_mask_grid
    local_portion = jnp.einsum(
        "anh,nkh->ank",
        remainder_rows.reshape(count, width // BLOCK, BLOCK),
        tiles,
        precision=HIGH_PRECISION,
    ).reshape(count, width)
    return local_portion + outer(right_projection, query_lookup)


def extend(update, targets, sep_total, has_update, bits, place):
    count = update.shape[0]
    pieces = 2 if has_update else 1
    rows = sep_total * pieces
    buffer = jnp.zeros((count, rows), jnp.float32).at[:, targets].add(update)
    if has_update:
        stack = jnp.stack([buffer[:, :sep_total], buffer[:, sep_total:]])
    else:
        stack = buffer[None]
    return group_extend(stack, bits, place)


def fetch(stack, targets, bits, place):
    front_full = group_fetch(stack, bits, place)
    rows = front_full.transpose(1, 0, 2).reshape(front_full.shape[1], -1)
    return jnp.take(rows, targets, axis=1)


def shards(
    source_leaf,
    block_leaf,
    expand_leaf,
    basis_leaf,
    pivot_leaf,
    couple_leaf,
    ranks_leaf,
    targets_leaf,
    source_middle,
    block_middle,
    expand_middle,
    basis_middle,
    pivot_middle,
    couple_middle,
    ranks_middle,
    targets_middle,
    source_upper,
    block_upper,
    expand_upper,
    basis_upper,
    pivot_upper,
    couple_upper,
    ranks_upper,
    targets_upper,
    source_root,
    block_root,
    expand_root,
    basis_root,
    pivot_root,
    ranks_root,
):
    levels = [
        (
            source_leaf,
            block_leaf,
            expand_leaf,
            basis_leaf,
            pivot_leaf,
            couple_leaf,
            ranks_leaf,
            targets_leaf,
        ),
        (
            source_middle,
            block_middle,
            expand_middle,
            basis_middle,
            pivot_middle,
            couple_middle,
            ranks_middle,
            targets_middle,
        ),
        (
            source_upper,
            block_upper,
            expand_upper,
            basis_upper,
            pivot_upper,
            couple_upper,
            ranks_upper,
            targets_upper,
        ),
        (source_root, block_root, expand_root, basis_root, pivot_root, None, ranks_root, None),
    ]
    leaves = lax.axis_size("leaf")
    across = lax.axis_size("grid")
    place = lax.axis_index("leaf")
    depth = leaves.bit_length() - 1
    groups = [1, leaves // 4, leaves // 2, leaves]
    bit_counts = [0, depth - 2, depth - 1, depth]
    owners = [place // groups[level] for level in range(4)]
    inc_sep = None
    inc_upd = None
    saved = []
    for level in range(4):
        source, block, expand, basis, pivot, couple, ranks, targets = levels[level]
        correction_entries, weight_entries, parts = forward_level(
            source, inc_sep, block, expand, basis, pivot, ranks, bit_counts[level], owners[level]
        )
        saved.append((correction_entries, parts))
        if level < 3:
            update = -outer(weight_entries, couple)
            if inc_upd is not None:
                update = update + inc_upd
            sep_total = levels[level + 1][0].shape[1] * across * groups[level + 1]
            has_update = level + 1 < 3
            stack = extend(update, targets, sep_total, has_update, bit_counts[level + 1], place)
            inc_sep = stack[0]
            inc_upd = stack[1] if has_update else None
    answers = [None, None, None, None]
    parent_stack = None
    for level in (3, 2, 1, 0):
        correction_entries, parts = saved[level]
        couple = levels[level][5]
        expand = levels[level][2]
        targets = levels[level][7]
        x_upd = None
        if level < 3:
            x_upd = fetch(parent_stack, targets, bit_counts[level + 1], place)
        xvals = backward_level(correction_entries, x_upd, couple, expand, parts, bit_counts[level])
        answers[level] = xvals
        if level > 0:
            parent_stack = xvals[None] if x_upd is None else jnp.stack([xvals, x_upd])
    return (answers[0], answers[1], answers[2], answers[3])


def solution(mesh):
    in_specs = (
        P(None, ("leaf", "grid")),
        P(("leaf", "grid"), None),
        P(("leaf", "grid"), None),
        P(("leaf", "grid"), None),
        P(("leaf", "grid")),
        P(("leaf", "grid"), None),
        P(),
        P(("leaf", "grid")),
        P(None, ("leaf", "grid")),
        P(("leaf", "grid"), None),
        P(("leaf", "grid"), None),
        P(("leaf", "grid"), None),
        P(("leaf", "grid")),
        P(("leaf", "grid"), None),
        P(),
        P(("leaf", "grid")),
        P(None, ("leaf", "grid")),
        P(("leaf", "grid"), None),
        P(("leaf", "grid"), None),
        P(("leaf", "grid"), None),
        P(("leaf", "grid")),
        P(("leaf", "grid"), None),
        P(),
        P(("leaf", "grid")),
        P(None, ("leaf", "grid")),
        P(("leaf", "grid"), None),
        P(("leaf", "grid"), None),
        P(("leaf", "grid"), None),
        P(("leaf", "grid")),
        P(),
    )
    out_specs = (
        P(None, ("leaf", "grid")),
        P(None, ("leaf", "grid")),
        P(None, ("leaf", "grid")),
        P(None, ("leaf", "grid")),
    )
    return jax.shard_map(shards, mesh=mesh, in_specs=in_specs, out_specs=out_specs, check_vma=False)
```

profile of v0, /device:TPU:0, one launch (start us, length us, event | category | flops | bytes accessed | tf_op | source)
XLA Modules:
  0.0 397.3 jit_solution(7661426514770940477)
XLA Ops:
  17.3 27.4 %all-reduce.5.cloned.1.call-done = f32[144,128]{1,0:T(8,128)} async-done(((f32[144,128]{1,0:T(8,128)}), f32[144,128]{1,0:T(8,128)}) %all-reduce.5.cloned.1.call-update) | async-done | bytes 73744 | tf_op jit(solution)/shard_map/psum | solution.py:42
  53.4 21.0 %reduce-scatter.4.cloned.1.call-done = f32[2,8,128]{2,1,0:T(8,128)} async-done(((f32[2,8,512]{2,1,0:T(8,128)}), f32[2,8,128]{2,1,0:T(8,128)}) %reduce-scatter.4.cloned.1.call-update) | async-done | bytes 8208 | tf_op jit(solution)/shard_map/reduce_scatter | solution.py:65
  77.7 29.1 %all-reduce.7.cloned.1.call-done = f32[144,128]{1,0:T(8,128)} async-done(((f32[144,128]{1,0:T(8,128)}), f32[144,128]{1,0:T(8,128)}) %all-reduce.7.cloned.1.call-update) | async-done | bytes 73744 | tf_op jit(solution)/shard_map/psum | solution.py:42
  128.0 21.2 %reduce-scatter.6.cloned.1.call-done = f32[2,8,128]{2,1,0:T(8,128)} async-done(((f32[2,8,512]{2,1,0:T(8,128)}), f32[2,8,128]{2,1,0:T(8,128)}) %reduce-scatter.6.cloned.1.call-update) | async-done | bytes 8208 | tf_op jit(solution)/shard_map/reduce_scatter | solution.py:65
  152.4 29.2 %all-reduce.9.cloned.1.call-done = f32[144,128]{1,0:T(8,128)} async-done(((f32[144,128]{1,0:T(8,128)}), f32[144,128]{1,0:T(8,128)}) %all-reduce.9.cloned.1.call-update) | async-done | bytes 73744 | tf_op jit(solution)/shard_map/psum | solution.py:42
  196.0 2.7 collective-permute-start.6
  198.7 2.8 collective-permute-done.6
  205.2 9.0 %collective-permute-done.7 = f32[1,8,1024]{1,2,0:T(8,128)S(1)} collective-permute-done((f32[1,8,1024]{1,2,0:T(8,128)S(1)}, f32[1,8,1024]{1,2,0:T(8,128)S(1)}, u32[]{:S(2)}, u32[]{:S(2)}) %collective-permute-start.7) | collective-permute-done | bytes 32800 | tf_op jit(solution)/shard_map/ppermute | solution.py:14
  216.7 4.2 %collective-permute-done.8 = f32[1,8,512]{1,2,0:T(8,128)S(1)} collective-permute-done((f32[1,8,512]{1,2,0:T(8,128)S(1)}, f32[1,8,512]{1,2,0:T(8,128)S(1)}, u32[]{:S(2)}, u32[]{:S(2)}) %collective-permute-start.8) | collective-permute-done | bytes 16416 | tf_op jit(solution)/shard_map/ppermute | solution.py:14
  222.3 20.4 %reduce-scatter.8.cloned.1.call-done = f32[1,8,128]{1,2,0:T(8,128)} async-done(((f32[1,8,512]{1,2,0:T(8,128)}), f32[1,8,128]{1,2,0:T(8,128)}) %reduce-scatter.8.cloned.1.call-update) | async-done | bytes 4112 | tf_op jit(solution)/shard_map/reduce_scatter | solution.py:65
  246.3 29.2 %all-reduce.11.cloned.1.call-done = f32[144,128]{1,0:T(8,128)} async-done(((f32[144,128]{1,0:T(8,128)}), f32[144,128]{1,0:T(8,128)}) %all-reduce.11.cloned.1.call-update) | async-done | bytes 73744 | tf_op jit(solution)/shard_map/psum | solution.py:42
  277.4 3.0 collective-permute-done.9
  283.1 2.6 collective-permute-done.10
  285.7 2.7 collective-permute-start.11
  288.5 2.5 collective-permute-done.11
  291.4 5.9 %psum.60 = f32[8,128]{1,0:T(8,128)S(1)} all-reduce(f32[8,128]{1,0:T(8,128)S(1)} %fusion.123), channel_id=1, replica_groups=mesh['leaf'=8,'grid'=4] {'grid'}, use_global_device_ids=true, to_apply=%region_10.11 | all-reduce | flops 1024 | bytes 8192 | tf_op jit(solution)/shard_map/psum | solution.py:42
  304.6 3.0 collective-permute-start.14
  309.4 5.6 %all-gather = f32[8,512]{1,0:T(8,128)S(1)} all-gather(f32[8,128]{1,0:T(8,128)S(1)} %convolution_add_fusion.3), channel_id=2, replica_groups=mesh['leaf'=8,'grid'=4] {'grid'}, dimensions={1}, use_global_device_ids=true | all-gather | bytes 20480 | tf_op jit(solution)/shard_map/all_gather | solution.py:69
  322.6 3.0 collective-permute-start.17
  330.0 5.8 %psum.61 = f32[16,128]{1,0:T(8,128)S(1)} all-reduce(f32[16,128]{1,0:T(8,128)S(1)} %pad_maximum_fusion.6), channel_id=1, replica_groups=mesh['leaf'=8,'grid'=4] {'grid'}, use_global_device_ids=true, to_apply=%region_11.13 | all-reduce | flops 2048 | bytes 16384 | tf_op jit(solution)/shard_map/psum | solution.py:42
  346.0 5.5 %all_gather.10 = f32[2,8,512]{2,1,0:T(8,128)S(1)} all-gather(f32[2,8,128]{2,1,0:T(8,128)S(1)} %pad_maximum_fusion.7), channel_id=1, replica_groups=mesh['leaf'=8,'grid'=4] {'grid'}, dimensions={2}, use_global_device_ids=true | all-gather | bytes 40960 | tf_op jit(solution)/shard_map/all_gather | solution.py:69
  361.3 5.8 %psum.62 = f32[16,128]{1,0:T(8,128)S(1)} all-reduce(f32[16,128]{1,0:T(8,128)S(1)} %pad_maximum_fusion.8), channel_id=1, replica_groups=mesh['leaf'=8,'grid'=4] {'grid'}, use_global_device_ids=true, to_apply=%region_12.14 | all-reduce | flops 2048 | bytes 16384 | tf_op jit(solution)/shard_map/psum | solution.py:42
  371.7 5.3 %all_gather.11 = f32[2,8,512]{2,1,0:T(8,128)S(1)} all-gather(f32[2,8,128]{2,1,0:T(8,128)S(1)} %pad_maximum_fusion.9), channel_id=1, replica_groups=mesh['leaf'=8,'grid'=4] {'grid'}, dimensions={2}, use_global_device_ids=true | all-gather | bytes 40960 | tf_op jit(solution)/shard_map/all_gather | solution.py:69
  382.4 6.5 %psum.63 = f32[16,128]{1,0:T(8,128)S(1)} all-reduce(f32[16,128]{1,0:T(8,128)S(1)} %pad_maximum_fusion.10), channel_id=1, replica_groups=mesh['leaf'=8,'grid'=4] {'grid'}, use_global_device_ids=true, to_apply=%region_13.15 | all-reduce | flops 2048 | bytes 16384 | tf_op jit(solution)/shard_map/psum | solution.py:42
  (304 shorter events, 128.9 us)
Async XLA Ops:
  7.2 37.5 %all-reduce.5.cloned.1.call-start = ((), (), s32[]{:S(2)}) async-start(), calls=%async_computation.3 | async-start | bytes 147456 | tf_op jit(solution)/shard_map/psum | solution.py:42
  12.1 62.3 %reduce-scatter.4.cloned.1.call-start = ((), (), s32[]{:S(2)}) async-start(), calls=%async_computation.4 | async-start | bytes 40960 | tf_op jit(solution)/shard_map/reduce_scatter | solution.py:65
  48.2 4.0 collective-permute-start
  52.8 54.0 %all-reduce.7.cloned.1.call-start = ((), (), s32[]{:S(2)}) async-start(), calls=%async_computation.5 | async-start | bytes 147456 | tf_op jit(solution)/shard_map/psum | solution.py:42
  77.0 72.3 %reduce-scatter.6.cloned.1.call-start = ((), (), s32[]{:S(2)}) async-start(), calls=%async_computation.6 | async-start | bytes 40960 | tf_op jit(solution)/shard_map/reduce_scatter | solution.py:65
  106.8 4.9 %collective-permute-start.1 = (f32[144,128]{1,0:T(8,128)}, f32[144,128]{1,0:T(8,128)S(1)}, u32[]{:S(2)}, u32[]{:S(2)}) collective-permute-start(f32[144,128]{1,0:T(8,128)} %all-reduce.7.cloned.1.call-done), channel_id=1, source_target_pairs={{0,4},{4,0},{8,12},{12,8},{16,20},{20,16},{24,28},{28,24},{1,5},{5... | collective-permute-start | bytes 221192 | tf_op jit(solution)/shard_map/ppermute | solution.py:14
  118.9 4.3 %collective-permute-start.2 = (f32[2,8,1024]{2,1,0:T(8,128)S(1)}, f32[2,8,1024]{2,1,0:T(8,128)S(1)}, u32[]{:S(2)}, u32[]{:S(2)}) collective-permute-start(f32[2,8,1024]{2,1,0:T(8,128)S(1)} %broadcast_select_fusion), channel_id=1, source_target_pairs={{0,8},{4,12},{8,0},{12,4},{16,24},{20,28},{24,16},{28,20},{1,9},{5... | collective-permute-start | bytes 196616 | tf_op jit(solution)/shard_map/ppermute | solution.py:14
  123.3 4.0 %collective-permute-start.3 = (f32[2,8,512]{2,1,0:T(8,128)S(1)}, f32[2,8,512]{2,1,0:T(8,128)S(1)}, u32[]{:S(2)}, u32[]{:S(2)}) collective-permute-start(f32[2,8,512]{2,1,0:T(8,128)S(1)} %slice_select_fusion.3), channel_id=1, source_target_pairs={{0,4},{4,0},{8,12},{12,8},{16,20},{20,16},{24,28},{28,24},{1,5},{5... | collective-permute-start | bytes 98312 | tf_op jit(solution)/shard_map/ppermute | solution.py:14
  127.9 53.7 %all-reduce.9.cloned.1.call-start = ((), (), s32[]{:S(2)}) async-start(), calls=%async_computation.7 | async-start | bytes 147456 | tf_op jit(solution)/shard_map/psum | solution.py:42
  151.8 90.8 %reduce-scatter.8.cloned.1.call-start = ((), (), s32[]{:S(2)}) async-start(), calls=%async_computation.8 | async-start | bytes 327680 | tf_op jit(solution)/shard_map/reduce_scatter | solution.py:65
  181.6 4.9 %collective-permute-start.4 = (f32[144,128]{1,0:T(8,128)}, f32[144,128]{1,0:T(8,128)S(1)}, u32[]{:S(2)}, u32[]{:S(2)}) collective-permute-start(f32[144,128]{1,0:T(8,128)} %all-reduce.9.cloned.1.call-done), channel_id=1, source_target_pairs={{0,4},{4,0},{8,12},{12,8},{16,20},{20,16},{24,28},{28,24},{1,5},{5... | collective-permute-start | bytes 221192 | tf_op jit(solution)/shard_map/ppermute | solution.py:14
  187.4 4.4 %collective-permute-start.5 = (f32[144,128]{1,0:T(8,128)S(1)}, f32[144,128]{1,0:T(8,128)S(1)}, u32[]{:S(2)}, u32[]{:S(2)}) collective-permute-start(f32[144,128]{1,0:T(8,128)S(1)} %add.207), channel_id=1, source_target_pairs={{0,8},{4,12},{8,0},{12,4},{16,24},{20,28},{24,16},{28,20},{1,9},{5... | collective-permute-start | bytes 221192 | tf_op jit(solution)/shard_map/ppermute | solution.py:14
  196.0 5.5 %collective-permute-start.6 = (f32[1,8,2048]{2,1,0:T(8,128)}, f32[1,8,2048]{2,1,0:T(8,128)}, u32[]{:S(2)}, u32[]{:S(2)}) collective-permute-start(f32[1,8,2048]{2,1,0:T(8,128)} %copy.65), channel_id=1, source_target_pairs={{0,16},{4,20},{8,24},{12,28},{16,0},{20,4},{24,8},{28,12},{1,17},{... | collective-permute-start | bytes 196616 | tf_op jit(solution)/shard_map/ppermute | solution.py:14
  203.0 11.2 %collective-permute-start.7 = (f32[1,8,1024]{1,2,0:T(8,128)S(1)}, f32[1,8,1024]{1,2,0:T(8,128)S(1)}, u32[]{:S(2)}, u32[]{:S(2)}) collective-permute-start(f32[1,8,1024]{1,2,0:T(8,128)S(1)} %slice_select_fusion.1), channel_id=1, source_target_pairs={{0,8},{4,12},{8,0},{12,4},{16,24},{20,28},{24,16},{28,20},{1,9},{5... | collective-permute-start | bytes 98312 | tf_op jit(solution)/shard_map/ppermute | solution.py:14
  214.4 6.4 %collective-permute-start.8 = (f32[1,8,512]{1,2,0:T(8,128)S(1)}, f32[1,8,512]{1,2,0:T(8,128)S(1)}, u32[]{:S(2)}, u32[]{:S(2)}) collective-permute-start(f32[1,8,512]{1,2,0:T(8,128)S(1)} %slice_select_fusion.2), channel_id=1, source_target_pairs={{0,4},{4,0},{8,12},{12,8},{16,20},{20,16},{24,28},{28,24},{1,5},{5... | collective-permute-start | bytes 49160 | tf_op jit(solution)/shard_map/ppermute | solution.py:14
  221.6 53.9 %all-reduce.11.cloned.1.call-start = ((), (), s32[]{:S(2)}) async-start(), calls=%async_computation.9 | async-start | bytes 147456 | tf_op jit(solution)/shard_map/psum | solution.py:42
  275.5 4.9 %collective-permute-start.9 = (f32[144,128]{1,0:T(8,128)}, f32[144,128]{1,0:T(8,128)S(1)}, u32[]{:S(2)}, u32[]{:S(2)}) collective-permute-start(f32[144,128]{1,0:T(8,128)} %all-reduce.11.cloned.1.call-done), channel_id=1, source_target_pairs={{0,4},{4,0},{8,12},{12,8},{16,20},{20,16},{24,28},{28,24},{1,5},{5... | collective-permute-start | bytes 221192 | tf_op jit(solution)/shard_map/ppermute | solution.py:14
  281.3 4.4 %collective-permute-start.10 = (f32[144,128]{1,0:T(8,128)S(1)}, f32[144,128]{1,0:T(8,128)S(1)}, u32[]{:S(2)}, u32[]{:S(2)}) collective-permute-start(f32[144,128]{1,0:T(8,128)S(1)} %add.219), channel_id=1, source_target_pairs={{0,8},{4,12},{8,0},{12,4},{16,24},{20,28},{24,16},{28,20},{1,9},{5... | collective-permute-start | bytes 221192 | tf_op jit(solution)/shard_map/ppermute | solution.py:14
  285.7 5.3 %collective-permute-start.11 = (f32[144,128]{1,0:T(8,128)S(1)}, f32[144,128]{1,0:T(8,128)S(1)}, u32[]{:S(2)}, u32[]{:S(2)}) collective-permute-start(f32[144,128]{1,0:T(8,128)S(1)} %add.220), channel_id=1, source_target_pairs={{0,16},{4,20},{8,24},{12,28},{16,0},{20,4},{24,8},{28,12},{1,17},{... | collective-permute-start | bytes 221192 | tf_op jit(solution)/shard_map/ppermute | solution.py:14
  304.6 4.6 %collective-permute-start.14 = (f32[8,128]{1,0:T(8,128)S(1)}, f32[8,128]{1,0:T(8,128)S(1)}, u32[]{:S(2)}, u32[]{:S(2)}) collective-permute-start(f32[8,128]{1,0:T(8,128)S(1)} %add.224), channel_id=1, source_target_pairs={{0,16},{4,20},{8,24},{12,28},{16,0},{20,4},{24,8},{28,12},{1,17},{... | collective-permute-start | bytes 12296 | tf_op jit(solution)/shard_map/ppermute | solution.py:14
  318.7 3.9 collective-permute-start.16
  322.6 5.2 %collective-permute-start.17 = (f32[1,8,2048]{2,1,0:T(8,128)S(1)}, f32[1,8,2048]{2,1,0:T(8,128)S(1)}, u32[]{:S(2)}, u32[]{:S(2)}) collective-permute-start(f32[1,8,2048]{2,1,0:T(8,128)S(1)} %maximum_select_fusion.2), channel_id=1, source_target_pairs={{0,16},{4,20},{8,24},{12,28},{16,0},{20,4},{24,8},{28,12},{1,17},{... | collective-permute-start | bytes 196616 | tf_op jit(solution)/shard_map/ppermute | solution.py:14
  351.5 3.9 collective-permute-start.20
  355.4 4.3 %collective-permute-start.21 = (f32[2,8,1024]{2,1,0:T(8,128)S(1)}, f32[2,8,1024]{2,1,0:T(8,128)S(1)}, u32[]{:S(2)}, u32[]{:S(2)}) collective-permute-start(f32[2,8,1024]{2,1,0:T(8,128)S(1)} %maximum_select_fusion.4), channel_id=1, source_target_pairs={{0,8},{4,12},{8,0},{12,4},{16,24},{20,28},{24,16},{28,20},{1,9},{5... | collective-permute-start | bytes 196616 | tf_op jit(solution)/shard_map/ppermute | solution.py:14
  (67 other events, 2687.7 us)
Sparse Core Ops, SparseCore 0:
  12.2 32.3 all-reduce.4
  52.9 21.4 reduce-scatter.3
  77.1 29.6 all-reduce.6
  128.0 21.1 reduce-scatter.5
  151.9 29.6 all-reduce.8
  221.7 20.8 reduce-scatter.7
  245.8 29.6 all-reduce.10
where the time goes:
time: 398 us; the launch traced here: 397 us
  waiting for transfers between devices  239 us (60%)
  starting transfers between devices  45.5 us (11%)
  blocking collectives  40.3 us (10%)
  matrix products  24 us (6%)
  other arithmetic  20.3 us (5%)
  between operations  15.1 us (4%)
  local copies, waits for them, and re-layouts  13.5 us (3%)
    psum x4, waiting for transfers between devices, paired_total(): summed = lax.psum(partial_value, 'grid')  115 us
    reduce_scatter x3, waiting for transfers between devices, group_extend(): return lax.psum_scatter(stack, 'grid', scatter_dimension=2, tiled=True)  62.6 us
    ppermute x24, waiting for transfers between devices, from_partner(): return lax.ppermute(value, axis, pairs)  60.9 us
    ppermute x24, starting transfers between devices, from_partner(): return lax.ppermute(value, axis, pairs)  45.2 us
    psum x4, blocking collectives, paired_total(): summed = lax.psum(partial_value, 'grid')  24 us
    all_gather x3, blocking collectives, group_fetch(): current = lax.all_gather(stack, 'grid', axis=2, tiled=True)  16.4 us
    dot_general x18, matrix products, mult(): jnp.dot(left, right, precision=HIGH_PRECISION, preferred_element_type=jnp...  8.73 us
  transfers between devices with their start and end apart: 31, of which 31 were waited for; matrix products, arithmetic and copies ran while one was open for 3% of the time, Pallas kernels for 0%

commit v1 on v0

--- a/solution.py
+++ b/solution.py
@@ -39,7 +39,9 @@
 
 
 def paired_total(partial_value, bits):
-    summed = lax.psum(partial_value, "grid")
+    summed = partial_value
+    for hop in (1, 2):
+        summed = summed + lax.ppermute(summed, "grid", [(dev, dev ^ hop) for dev in range(4)])
     for bit in range(bits):
         summed = summed + from_partner(summed, "leaf", bit)
     return summed

time: 398 us -> 284 us (0.71)
  waiting for transfers between devices: 239 us -> 158 us
  blocking collectives: 40.3 us -> 15.8 us
  other arithmetic: 20.3 us -> 12.2 us
  matrix products: 24 us -> 19.9 us
    psum x4 -> x0, waiting for transfers between devices: 115 us -> none  [paired_total(): summed = lax.psum(partial_value, 'grid')]
    ppermute x0 -> x16, waiting for transfers between devices: none -> 33.3 us  [paired_total(): lax.ppermute(summed, 'grid', [(dev, dev ^ hop) for dev in range(4)])]
    psum x4 -> x0, blocking collectives: 24 us -> none  [paired_total(): summed = lax.psum(partial_value, 'grid')]
    ppermute x0 -> x16, starting transfers between devices: none -> 6.56 us  [paired_total(): lax.ppermute(summed, 'grid', [(dev, dev ^ hop) for dev in range(4)])]
  transfers between devices with their start and end apart: 31 -> 43, of which waited for: 31 -> 42; matrix products, arithmetic and copies ran while one was open for 3% -> 4% of each run, Pallas kernels for 0% -> 0%
where the time goes in v1:
time: 284 us
  waiting for transfers between devices  158 us (56%)
  starting transfers between devices  49 us (17%)
  matrix products  19.9 us (7%)
  blocking collectives  15.8 us (6%)
  between operations  14.9 us (5%)
  local copies, waits for them, and re-layouts  13.9 us (5%)
  other arithmetic  12.2 us (4%)
    ppermute x24, waiting for transfers between devices, from_partner(): return lax.ppermute(value, axis, pairs)  63.5 us
    reduce_scatter x3, waiting for transfers between devices, group_extend(): return lax.psum_scatter(stack, 'grid', scatter_dimension=2, tiled=True)  61 us
    ppermute x24, starting transfers between devices, from_partner(): return lax.ppermute(value, axis, pairs)  42.3 us
    ppermute x16, waiting for transfers between devices, paired_total(): lax.ppermute(summed, 'grid', [(dev, dev ^ hop) for dev in range(4)])  33.3 us
    all_gather x3, blocking collectives, group_fetch(): current = lax.all_gather(stack, 'grid', axis=2, tiled=True)  15.8 us
    dot_general x18, matrix products, mult(): jnp.dot(left, right, precision=HIGH_PRECISION, preferred_element_type=jnp...  7.23 us
    ppermute x16, starting transfers between devices, paired_total(): lax.ppermute(summed, 'grid', [(dev, dev ^ hop) for dev in range(4)])  6.56 us
  transfers between devices with their start and end apart: 43, of which 42 were waited for; matrix products, arithmetic and copies ran while one was open for 4% of the time, Pallas kernels for 0%

profile of v1, /device:TPU:0, one launch (start us, length us, event | category | flops | bytes accessed | tf_op | source)
XLA Modules:
  0.0 283.6 jit_solution(15736979826174918743)
XLA Ops:
  15.8 2.6 collective-permute-start.1
  29.3 21.0 %reduce-scatter.4.cloned.1.call-done = f32[2,8,128]{2,1,0:T(8,128)} async-done(((f32[2,8,512]{2,1,0:T(8,128)}), f32[2,8,128]{2,1,0:T(8,128)}) %reduce-scatter.4.cloned.1.call-update) | async-done | bytes 8208 | tf_op jit(solution)/shard_map/reduce_scatter | solution.py:67
  54.4 3.5 %collective-permute-done.4 = f32[144,128]{1,0:T(8,128)S(1)} collective-permute-done((f32[144,128]{1,0:T(8,128)S(1)}, f32[144,128]{1,0:T(8,128)S(1)}, u32[]{:S(2)}, u32[]{:S(2)}) %collective-permute-start.4) | collective-permute-done | bytes 73760 | tf_op jit(solution)/shard_map/ppermute | solution.py:44
  70.2 2.8 collective-permute-done.6
  77.8 19.6 %reduce-scatter.6.cloned.1.call-done = f32[2,8,128]{2,1,0:T(8,128)} async-done(((f32[2,8,512]{2,1,0:T(8,128)}), f32[2,8,128]{2,1,0:T(8,128)}) %reduce-scatter.6.cloned.1.call-update) | async-done | bytes 8208 | tf_op jit(solution)/shard_map/reduce_scatter | solution.py:67
  101.4 3.6 %collective-permute-done.9 = f32[144,128]{1,0:T(8,128)S(1)} collective-permute-done((f32[144,128]{1,0:T(8,128)S(1)}, f32[144,128]{1,0:T(8,128)S(1)}, u32[]{:S(2)}, u32[]{:S(2)}) %collective-permute-start.9) | collective-permute-done | bytes 73760 | tf_op jit(solution)/shard_map/ppermute | solution.py:44
  118.1 2.4 collective-permute-start.12
  120.5 3.1 %collective-permute-done.12 = f32[1,8,2048]{2,1,0:T(8,128)} collective-permute-done((f32[1,8,2048]{2,1,0:T(8,128)}, f32[1,8,2048]{2,1,0:T(8,128)}, u32[]{:S(2)}, u32[]{:S(2)}) %collective-permute-start.12) | collective-permute-done | bytes 65568 | tf_op jit(solution)/shard_map/ppermute | solution.py:14
  126.6 8.1 %collective-permute-done.13 = f32[1,8,1024]{1,2,0:T(8,128)S(1)} collective-permute-done((f32[1,8,1024]{1,2,0:T(8,128)S(1)}, f32[1,8,1024]{1,2,0:T(8,128)S(1)}, u32[]{:S(2)}, u32[]{:S(2)}) %collective-permute-start.13) | collective-permute-done | bytes 32800 | tf_op jit(solution)/shard_map/ppermute | solution.py:14
  136.5 4.9 %collective-permute-done.14 = f32[1,8,512]{1,2,0:T(8,128)S(1)} collective-permute-done((f32[1,8,512]{1,2,0:T(8,128)S(1)}, f32[1,8,512]{1,2,0:T(8,128)S(1)}, u32[]{:S(2)}, u32[]{:S(2)}) %collective-permute-start.14) | collective-permute-done | bytes 16416 | tf_op jit(solution)/shard_map/ppermute | solution.py:14
  142.6 20.5 %reduce-scatter.8.cloned.1.call-done = f32[1,8,128]{1,2,0:T(8,128)} async-done(((f32[1,8,512]{1,2,0:T(8,128)}), f32[1,8,128]{1,2,0:T(8,128)}) %reduce-scatter.8.cloned.1.call-update) | async-done | bytes 4112 | tf_op jit(solution)/shard_map/reduce_scatter | solution.py:67
  167.2 4.0 %collective-permute-done.16 = f32[144,128]{1,0:T(8,128)S(1)} collective-permute-done((f32[144,128]{1,0:T(8,128)S(1)}, f32[144,128]{1,0:T(8,128)S(1)}, u32[]{:S(2)}, u32[]{:S(2)}) %collective-permute-start.16) | collective-permute-done | bytes 73760 | tf_op jit(solution)/shard_map/ppermute | solution.py:44
  172.8 2.9 %collective-permute-done.17 = f32[144,128]{1,0:T(8,128)S(1)} collective-permute-done((f32[144,128]{1,0:T(8,128)S(1)}, f32[144,128]{1,0:T(8,128)S(1)}, u32[]{:S(2)}, u32[]{:S(2)}) %collective-permute-start.17) | collective-permute-done | bytes 73760 | tf_op jit(solution)/shard_map/ppermute | solution.py:14
  177.2 2.9 %collective-permute-done.18 = f32[144,128]{1,0:T(8,128)S(1)} collective-permute-done((f32[144,128]{1,0:T(8,128)S(1)}, f32[144,128]{1,0:T(8,128)S(1)}, u32[]{:S(2)}, u32[]{:S(2)}) %collective-permute-start.18) | collective-permute-done | bytes 73760 | tf_op jit(solution)/shard_map/ppermute | solution.py:14
  180.2 3.1 %collective-permute-start.19 = (f32[144,128]{1,0:T(8,128)S(1)}, f32[144,128]{1,0:T(8,128)S(1)}, u32[]{:S(2)}, u32[]{:S(2)}) collective-permute-start(f32[144,128]{1,0:T(8,128)S(1)} %add.260), channel_id=1, source_target_pairs={{0,16},{4,20},{8,24},{12,28},{16,0},{20,4},{24,8},{28,12},{1,17},{... | collective-permute-start | bytes 221192 | tf_op jit(solution)/shard_map/ppermute | solution.py:14
  187.7 3.0 %collective-permute-done.21 = f32[8,128]{1,0:T(8,128)S(1)} collective-permute-done((f32[8,128]{1,0:T(8,128)S(1)}, f32[8,128]{1,0:T(8,128)S(1)}, u32[]{:S(2)}, u32[]{:S(2)}) %collective-permute-start.21) | collective-permute-done | bytes 4128 | tf_op jit(solution)/shard_map/ppermute | solution.py:44
  198.0 3.0 %collective-permute-start.24 = (f32[8,128]{1,0:T(8,128)S(1)}, f32[8,128]{1,0:T(8,128)S(1)}, u32[]{:S(2)}, u32[]{:S(2)}) collective-permute-start(f32[8,128]{1,0:T(8,128)S(1)} %add.266), channel_id=1, source_target_pairs={{0,16},{4,20},{8,24},{12,28},{16,0},{20,4},{24,8},{28,12},{1,17},{... | collective-permute-start | bytes 12296 | tf_op jit(solution)/shard_map/ppermute | solution.py:14
  202.8 5.4 %all-gather = f32[8,512]{1,0:T(8,128)S(1)} all-gather(f32[8,128]{1,0:T(8,128)S(1)} %convolution_add_fusion.3), channel_id=2, replica_groups=mesh['leaf'=8,'grid'=4] {'grid'}, dimensions={1}, use_global_device_ids=true | all-gather | bytes 20480 | tf_op jit(solution)/shard_map/all_gather | solution.py:71
  215.8 3.0 %collective-permute-start.27 = (f32[1,8,2048]{2,1,0:T(8,128)S(1)}, f32[1,8,2048]{2,1,0:T(8,128)S(1)}, u32[]{:S(2)}, u32[]{:S(2)}) collective-permute-start(f32[1,8,2048]{2,1,0:T(8,128)S(1)} %maximum_select_fusion.2), channel_id=1, source_target_pairs={{0,16},{4,20},{8,24},{12,28},{16,0},{20,4},{24,8},{28,12},{1,17},{... | collective-permute-start | bytes 196616 | tf_op jit(solution)/shard_map/ppermute | solution.py:14
  224.4 3.1 %collective-permute-done.29 = f32[16,128]{1,0:T(8,128)S(1)} collective-permute-done((f32[16,128]{1,0:T(8,128)S(1)}, f32[16,128]{1,0:T(8,128)S(1)}, u32[]{:S(2)}, u32[]{:S(2)}) %collective-permute-start.29) | collective-permute-done | bytes 8224 | tf_op jit(solution)/shard_map/ppermute | solution.py:44
  235.7 5.2 %all_gather.10 = f32[2,8,512]{2,1,0:T(8,128)S(1)} all-gather(f32[2,8,128]{2,1,0:T(8,128)S(1)} %pad_maximum_fusion.7), channel_id=1, replica_groups=mesh['leaf'=8,'grid'=4] {'grid'}, dimensions={2}, use_global_device_ids=true | all-gather | bytes 40960 | tf_op jit(solution)/shard_map/all_gather | solution.py:71
  252.7 2.9 %collective-permute-done.35 = f32[16,128]{1,0:T(8,128)S(1)} collective-permute-done((f32[16,128]{1,0:T(8,128)S(1)}, f32[16,128]{1,0:T(8,128)S(1)}, u32[]{:S(2)}, u32[]{:S(2)}) %collective-permute-start.35) | collective-permute-done | bytes 8224 | tf_op jit(solution)/shard_map/ppermute | solution.py:44
  260.1 5.2 %all_gather.11 = f32[2,8,512]{2,1,0:T(8,128)S(1)} all-gather(f32[2,8,128]{2,1,0:T(8,128)S(1)} %pad_maximum_fusion.9), channel_id=1, replica_groups=mesh['leaf'=8,'grid'=4] {'grid'}, dimensions={2}, use_global_device_ids=true | all-gather | bytes 40960 | tf_op jit(solution)/shard_map/all_gather | solution.py:71
  272.5 3.1 %collective-permute-done.39 = f32[16,128]{1,0:T(8,128)S(1)} collective-permute-done((f32[16,128]{1,0:T(8,128)S(1)}, f32[16,128]{1,0:T(8,128)S(1)}, u32[]{:S(2)}, u32[]{:S(2)}) %collective-permute-start.39) | collective-permute-done | bytes 8224 | tf_op jit(solution)/shard_map/ppermute | solution.py:44
  (337 shorter events, 130.0 us)
Async XLA Ops:
  7.2 43.1 %reduce-scatter.4.cloned.1.call-start = ((), (), s32[]{:S(2)}) async-start(), calls=%async_computation.3 | async-start | bytes 40960 | tf_op jit(solution)/shard_map/reduce_scatter | solution.py:67
  11.5 4.3 %collective-permute-start = (f32[144,128]{1,0:T(8,128)S(1)}, f32[144,128]{1,0:T(8,128)S(1)}, u32[]{:S(2)}, u32[]{:S(2)}) collective-permute-start(f32[144,128]{1,0:T(8,128)S(1)} %pad_maximum_fusion), channel_id=1, source_target_pairs={{0,1},{1,0},{2,3},{3,2},{4,5},{5,4},{6,7},{7,6},{8,9},{9,8},{10,11... | collective-permute-start | bytes 221192 | tf_op jit(solution)/shard_map/ppermute | solution.py:44
  15.8 5.5 %collective-permute-start.1 = (f32[144,128]{1,0:T(8,128)S(1)}, f32[144,128]{1,0:T(8,128)S(1)}, u32[]{:S(2)}, u32[]{:S(2)}) collective-permute-start(f32[144,128]{1,0:T(8,128)S(1)} %fusion.129), channel_id=1, source_target_pairs={{0,2},{1,3},{2,0},{3,1},{4,6},{5,7},{6,4},{7,5},{8,10},{9,11},{10,... | collective-permute-start | bytes 221192 | tf_op jit(solution)/shard_map/ppermute | solution.py:44
  24.5 4.0 %collective-permute-start.2 = (f32[2,8,512]{2,1,0:T(8,128)S(1)}, f32[2,8,512]{2,1,0:T(8,128)S(1)}, u32[]{:S(2)}, u32[]{:S(2)}) collective-permute-start(f32[2,8,512]{2,1,0:T(8,128)S(1)} %broadcast_select_fusion.1), channel_id=1, source_target_pairs={{0,4},{4,0},{8,12},{12,8},{16,20},{20,16},{24,28},{28,24},{1,5},{5... | collective-permute-start | bytes 98312 | tf_op jit(solution)/shard_map/ppermute | solution.py:14
  29.1 68.2 %reduce-scatter.6.cloned.1.call-start = ((), (), s32[]{:S(2)}) async-start(), calls=%async_computation.4 | async-start | bytes 40960 | tf_op jit(solution)/shard_map/reduce_scatter | solution.py:67
  53.5 4.4 %collective-permute-start.4 = (f32[144,128]{1,0:T(8,128)S(1)}, f32[144,128]{1,0:T(8,128)S(1)}, u32[]{:S(2)}, u32[]{:S(2)}) collective-permute-start(f32[144,128]{1,0:T(8,128)S(1)} %fusion.128), channel_id=1, source_target_pairs={{0,2},{1,3},{2,0},{3,1},{4,6},{5,7},{6,4},{7,5},{8,10},{9,11},{10,... | collective-permute-start | bytes 221192 | tf_op jit(solution)/shard_map/ppermute | solution.py:44
  57.9 4.4 %collective-permute-start.5 = (f32[144,128]{1,0:T(8,128)S(1)}, f32[144,128]{1,0:T(8,128)S(1)}, u32[]{:S(2)}, u32[]{:S(2)}) collective-permute-start(f32[144,128]{1,0:T(8,128)S(1)} %add.232), channel_id=1, source_target_pairs={{0,4},{4,0},{8,12},{12,8},{16,20},{20,16},{24,28},{28,24},{1,5},{5... | collective-permute-start | bytes 221192 | tf_op jit(solution)/shard_map/ppermute | solution.py:14
  68.7 4.3 %collective-permute-start.6 = (f32[2,8,1024]{2,1,0:T(8,128)S(1)}, f32[2,8,1024]{2,1,0:T(8,128)S(1)}, u32[]{:S(2)}, u32[]{:S(2)}) collective-permute-start(f32[2,8,1024]{2,1,0:T(8,128)S(1)} %broadcast_select_fusion), channel_id=1, source_target_pairs={{0,8},{4,12},{8,0},{12,4},{16,24},{20,28},{24,16},{28,20},{1,9},{5... | collective-permute-start | bytes 196616 | tf_op jit(solution)/shard_map/ppermute | solution.py:14
  73.1 4.0 %collective-permute-start.7 = (f32[2,8,512]{2,1,0:T(8,128)S(1)}, f32[2,8,512]{2,1,0:T(8,128)S(1)}, u32[]{:S(2)}, u32[]{:S(2)}) collective-permute-start(f32[2,8,512]{2,1,0:T(8,128)S(1)} %slice_select_fusion.3), channel_id=1, source_target_pairs={{0,4},{4,0},{8,12},{12,8},{16,20},{20,16},{24,28},{28,24},{1,5},{5... | collective-permute-start | bytes 98312 | tf_op jit(solution)/shard_map/ppermute | solution.py:14
  77.7 85.3 %reduce-scatter.8.cloned.1.call-start = ((), (), s32[]{:S(2)}) async-start(), calls=%async_computation.5 | async-start | bytes 327680 | tf_op jit(solution)/shard_map/reduce_scatter | solution.py:67
  100.6 4.4 %collective-permute-start.9 = (f32[144,128]{1,0:T(8,128)S(1)}, f32[144,128]{1,0:T(8,128)S(1)}, u32[]{:S(2)}, u32[]{:S(2)}) collective-permute-start(f32[144,128]{1,0:T(8,128)S(1)} %fusion.127), channel_id=1, source_target_pairs={{0,2},{1,3},{2,0},{3,1},{4,6},{5,7},{6,4},{7,5},{8,10},{9,11},{10,... | collective-permute-start | bytes 221192 | tf_op jit(solution)/shard_map/ppermute | solution.py:44
  105.0 4.4 %collective-permute-start.10 = (f32[144,128]{1,0:T(8,128)S(1)}, f32[144,128]{1,0:T(8,128)S(1)}, u32[]{:S(2)}, u32[]{:S(2)}) collective-permute-start(f32[144,128]{1,0:T(8,128)S(1)} %add.244), channel_id=1, source_target_pairs={{0,4},{4,0},{8,12},{12,8},{16,20},{20,16},{24,28},{28,24},{1,5},{5... | collective-permute-start | bytes 221192 | tf_op jit(solution)/shard_map/ppermute | solution.py:14
  109.4 4.4 %collective-permute-start.11 = (f32[144,128]{1,0:T(8,128)S(1)}, f32[144,128]{1,0:T(8,128)S(1)}, u32[]{:S(2)}, u32[]{:S(2)}) collective-permute-start(f32[144,128]{1,0:T(8,128)S(1)} %add.245), channel_id=1, source_target_pairs={{0,8},{4,12},{8,0},{12,4},{16,24},{20,28},{24,16},{28,20},{1,9},{5... | collective-permute-start | bytes 221192 | tf_op jit(solution)/shard_map/ppermute | solution.py:14
  118.1 5.5 %collective-permute-start.12 = (f32[1,8,2048]{2,1,0:T(8,128)}, f32[1,8,2048]{2,1,0:T(8,128)}, u32[]{:S(2)}, u32[]{:S(2)}) collective-permute-start(f32[1,8,2048]{2,1,0:T(8,128)} %copy.65), channel_id=1, source_target_pairs={{0,16},{4,20},{8,24},{12,28},{16,0},{20,4},{24,8},{28,12},{1,17},{... | collective-permute-start | bytes 196616 | tf_op jit(solution)/shard_map/ppermute | solution.py:14
  125.0 9.7 %collective-permute-start.13 = (f32[1,8,1024]{1,2,0:T(8,128)S(1)}, f32[1,8,1024]{1,2,0:T(8,128)S(1)}, u32[]{:S(2)}, u32[]{:S(2)}) collective-permute-start(f32[1,8,1024]{1,2,0:T(8,128)S(1)} %slice_select_fusion.1), channel_id=1, source_target_pairs={{0,8},{4,12},{8,0},{12,4},{16,24},{20,28},{24,16},{28,20},{1,9},{5... | collective-permute-start | bytes 98312 | tf_op jit(solution)/shard_map/ppermute | solution.py:14
  134.9 6.4 %collective-permute-start.14 = (f32[1,8,512]{1,2,0:T(8,128)S(1)}, f32[1,8,512]{1,2,0:T(8,128)S(1)}, u32[]{:S(2)}, u32[]{:S(2)}) collective-permute-start(f32[1,8,512]{1,2,0:T(8,128)S(1)} %slice_select_fusion.2), channel_id=1, source_target_pairs={{0,4},{4,0},{8,12},{12,8},{16,20},{20,16},{24,28},{28,24},{1,5},{5... | collective-permute-start | bytes 49160 | tf_op jit(solution)/shard_map/ppermute | solution.py:14
  166.8 4.4 %collective-permute-start.16 = (f32[144,128]{1,0:T(8,128)S(1)}, f32[144,128]{1,0:T(8,128)S(1)}, u32[]{:S(2)}, u32[]{:S(2)}) collective-permute-start(f32[144,128]{1,0:T(8,128)S(1)} %fusion.126), channel_id=1, source_target_pairs={{0,2},{1,3},{2,0},{3,1},{4,6},{5,7},{6,4},{7,5},{8,10},{9,11},{10,... | collective-permute-start | bytes 221192 | tf_op jit(solution)/shard_map/ppermute | solution.py:44
  171.2 4.4 %collective-permute-start.17 = (f32[144,128]{1,0:T(8,128)S(1)}, f32[144,128]{1,0:T(8,128)S(1)}, u32[]{:S(2)}, u32[]{:S(2)}) collective-permute-start(f32[144,128]{1,0:T(8,128)S(1)} %add.258), channel_id=1, source_target_pairs={{0,4},{4,0},{8,12},{12,8},{16,20},{20,16},{24,28},{28,24},{1,5},{5... | collective-permute-start | bytes 221192 | tf_op jit(solution)/shard_map/ppermute | solution.py:14
  175.7 4.4 %collective-permute-start.18 = (f32[144,128]{1,0:T(8,128)S(1)}, f32[144,128]{1,0:T(8,128)S(1)}, u32[]{:S(2)}, u32[]{:S(2)}) collective-permute-start(f32[144,128]{1,0:T(8,128)S(1)} %add.259), channel_id=1, source_target_pairs={{0,8},{4,12},{8,0},{12,4},{16,24},{20,28},{24,16},{28,20},{1,9},{5... | collective-permute-start | bytes 221192 | tf_op jit(solution)/shard_map/ppermute | solution.py:14
  180.2 5.4 %collective-permute-start.19 = (f32[144,128]{1,0:T(8,128)S(1)}, f32[144,128]{1,0:T(8,128)S(1)}, u32[]{:S(2)}, u32[]{:S(2)}) collective-permute-start(f32[144,128]{1,0:T(8,128)S(1)} %add.260), channel_id=1, source_target_pairs={{0,16},{4,20},{8,24},{12,28},{16,0},{20,4},{24,8},{28,12},{1,17},{... | collective-permute-start | bytes 221192 | tf_op jit(solution)/shard_map/ppermute | solution.py:14
  198.0 4.6 %collective-permute-start.24 = (f32[8,128]{1,0:T(8,128)S(1)}, f32[8,128]{1,0:T(8,128)S(1)}, u32[]{:S(2)}, u32[]{:S(2)}) collective-permute-start(f32[8,128]{1,0:T(8,128)S(1)} %add.266), channel_id=1, source_target_pairs={{0,16},{4,20},{8,24},{12,28},{16,0},{20,4},{24,8},{28,12},{1,17},{... | collective-permute-start | bytes 12296 | tf_op jit(solution)/shard_map/ppermute | solution.py:14
  211.9 3.9 %collective-permute-start.26 = (f32[1,8,1024]{2,1,0:T(8,128)S(1)}, f32[1,8,1024]{2,1,0:T(8,128)S(1)}, u32[]{:S(2)}, u32[]{:S(2)}) collective-permute-start(f32[1,8,1024]{2,1,0:T(8,128)S(1)} %maximum_select_fusion.6), channel_id=1, source_target_pairs={{0,8},{4,12},{8,0},{12,4},{16,24},{20,28},{24,16},{28,20},{1,9},{5... | collective-permute-start | bytes 98312 | tf_op jit(solution)/shard_map/ppermute | solution.py:14
  215.8 5.2 %collective-permute-start.27 = (f32[1,8,2048]{2,1,0:T(8,128)S(1)}, f32[1,8,2048]{2,1,0:T(8,128)S(1)}, u32[]{:S(2)}, u32[]{:S(2)}) collective-permute-start(f32[1,8,2048]{2,1,0:T(8,128)S(1)} %maximum_select_fusion.2), channel_id=1, source_target_pairs={{0,16},{4,20},{8,24},{12,28},{16,0},{20,4},{24,8},{28,12},{1,17},{... | collective-permute-start | bytes 196616 | tf_op jit(solution)/shard_map/ppermute | solution.py:14
  244.8 4.3 %collective-permute-start.33 = (f32[2,8,1024]{2,1,0:T(8,128)S(1)}, f32[2,8,1024]{2,1,0:T(8,128)S(1)}, u32[]{:S(2)}, u32[]{:S(2)}) collective-permute-start(f32[2,8,1024]{2,1,0:T(8,128)S(1)} %maximum_select_fusion.4), channel_id=1, source_target_pairs={{0,8},{4,12},{8,0},{12,4},{16,24},{20,28},{24,16},{28,20},{1,9},{5... | collective-permute-start | bytes 196616 | tf_op jit(solution)/shard_map/ppermute | solution.py:14
  (79 other events, 2036.5 us)
Sparse Core Ops, SparseCore 0:
  29.2 20.9 reduce-scatter.3
  77.8 19.5 reduce-scatter.5
  142.3 20.7 reduce-scatter.7
